TPU v7x, 32 devices: a whole 2x2x4 slice. The times are simulated.
32 devices in a mesh: hi: 4 (over y, core), lo: 8 (over z, x).
Axes of the slice: x: 2, y: 2, z: 4, core: 2. Of those that a mesh axis runs over, the one named last changes fastest.
Arguments:
- grm: bfloat16 [4, 8, 64, 4, 512], P(None, 'lo', None, 'hi'), as said below
- right_sides: float32 [2048, 512], P(('hi', 'lo')), may hold values from -6 to 6
- inv_diag: float32 [2048], P(('hi', 'lo')), may hold values from 0.3 to 1
- bases: float32 [2048, 576], P(('hi', 'lo')), may hold values from -0.75 to 0.75
- couplings: float32 [9, 64, 64], replicated, as said below
- level_map: int32 [8], replicated, may hold values from 0 to 7, each once
- variance: float32 [2], replicated, may hold values from 0.3 to 1.5
- iters_per_column: int32 [512], replicated, may hold values from 1 to 3
Outputs:
- solution: float32 [2048, 512], P(('hi', 'lo'))
- residual: float32 [2048, 512], P(('hi', 'lo'))
Inputs may be any that keep to these rules, and one draw needn't show every extreme that they name: `grm`: G is symmetric and positive definite. `couplings`: each of the 9 matrices is symmetric and positive definite. `level_map`: a permutation of the levels.
All inputs are finite; a program needn't handle non-finite values.
Results may differ from a plain program's by a relative error of at most 0.0055.
Values may be sent and summed in bfloat16 or wider, within the bound.
A program may use at most 64 MiB of HBM per device.

v0:
```python
import jax
import jax.numpy as jnp
from jax import lax
from jax.sharding import PartitionSpec as P

ITERS = 3


def from_partner(value, axis, bit):
    mask = 2**bit
    pairs = [(source, source ^ mask) for source in range(lax.axis_size(axis))]
    return lax.ppermute(value, axis, pairs)


def level_pieces(coefficients, couplings, level):
    level_ids = jnp.arange(couplings.shape[0], dtype=jnp.int32)
    select = (level_ids == level).astype(jnp.float32)
    own_part = jnp.einsum("l,lrb->rb", select, coefficients)
    matrix = jnp.einsum("l,lrs->rs", select, couplings)
    return (own_part, matrix, select)


def add_level(stacked, own_part, other_part, matrix, select):
    term = jnp.dot(matrix, own_part + other_part, precision=lax.Precision.HIGHEST)
    return stacked + select[:, None, None] * term[None]


def local(grm, right_sides, inv_diag, bases, couplings, level_map, variance, iters_per_column):
    row_count, column_count = right_sides.shape
    grm_block = grm.reshape(-1, grm.shape[4])
    level_total = couplings.shape[0]
    rank_width = couplings.shape[1]
    lo_bits = lax.axis_size("lo").bit_length() - 1
    hi_bits = lax.axis_size("hi").bit_length() - 1
    genetic = variance[0]
    noise = variance[1]

    def precondition(resid):
        coefficients = lax.dot_general(
            bases, resid, (((0,), (0,)), ((), ())), precision=lax.Precision.HIGHEST
        )
        coefficients = coefficients.reshape(level_total, rank_width, column_count)
        stacked = jnp.zeros((level_total - 1, rank_width, column_count), jnp.float32)
        for bit_index in range(lo_bits):
            own_part, matrix, select = level_pieces(coefficients, couplings, level_map[bit_index])
            other_part = from_partner(own_part.astype(jnp.bfloat16), "lo", bit_index).astype(
                own_part.dtype
            )
            stacked = add_level(stacked, own_part, other_part, matrix, select[: level_total - 1])
        for bit_index in range(hi_bits):
            own_part, matrix, select = level_pieces(
                coefficients, couplings, level_map[lo_bits + bit_index]
            )
            other_part = from_partner(own_part.astype(jnp.bfloat16), "hi", bit_index).astype(
                own_part.dtype
            )
            stacked = add_level(stacked, own_part, other_part, matrix, select[: level_total - 1])
        split_at = (level_total - 1) * rank_width
        local_part = inv_diag[:, None] * resid + jnp.dot(
            bases[:, :split_at],
            stacked.reshape(split_at, column_count),
            precision=lax.Precision.HIGHEST,
        )
        coarse_basis = bases[:, split_at:]
        partial_energy = jnp.sum(resid * local_part, axis=0)
        total, summed_energy = lax.psum(
            (coefficients[level_total - 1], partial_energy), ("hi", "lo")
        )
        coarse = jnp.dot(couplings[level_total - 1], total, precision=lax.Precision.HIGHEST)
        scaled = local_part + jnp.dot(coarse_basis, coarse, precision=lax.Precision.HIGHEST)
        energy = summed_energy + jnp.sum(total * coarse, axis=0)
        return (scaled, energy)

    solution = jnp.zeros_like(right_sides)
    residual = right_sides
    scaled, energy = precondition(residual)
    direction = scaled
    for step in range(ITERS):
        rounded = direction.astype(jnp.bfloat16)
        partial_value = jnp.dot(
            grm_block,
            lax.all_gather(rounded, "lo", axis=0, tiled=True),
            preferred_element_type=jnp.float32,
        )
        product = lax.psum_scatter(partial_value, "hi", scatter_dimension=0, tiled=True)
        image = genetic * product + noise * direction
        curvature = lax.psum(jnp.sum(direction * image, axis=0), ("hi", "lo"))
        alpha = energy / curvature
        stepsize = jnp.where(step < iters_per_column, alpha, jnp.zeros_like(alpha))
        solution = solution + stepsize * direction
        residual = residual - stepsize * image
        if step + 1 < ITERS:
            scaled, fresh = precondition(residual)
            direction = scaled + fresh / energy * direction
            energy = fresh
    return (solution, residual)


def solution(mesh):
    in_specs = (
        P(None, "lo", None, "hi", None),
        P(("hi", "lo"), None),
        P(("hi", "lo")),
        P(("hi", "lo"), None),
        P(),
        P(),
        P(),
        P(),
    )
    out_specs = (P(("hi", "lo"), None), P(("hi", "lo"), None))
    return jax.shard_map(local, mesh=mesh, in_specs=in_specs, out_specs=out_specs, check_vma=False)
```

profile of v0, /device:TPU:0, one launch (start us, length us, event | category | flops | bytes accessed | tf_op | source)
XLA Modules:
  0.0 806.3 jit_solution(18174941709177877963)
XLA Ops:
  7.2 1.5 fusion.146
  8.7 2.1 fusion.150
  10.8 1.3 fusion.26
  12.1 3.1 collective-permute-start.1
  15.3 1.4 fusion.24
  16.6 2.7 collective-permute-start.2
  19.3 1.4 fusion.22
  20.8 1.4 fusion.20
  22.1 1.6 collective-permute-start.4
  23.7 1.4 fusion.28
  25.1 1.6 collective-permute-start
  30.6 0.9 fusion.58
  31.5 0.9 fusion.54
  32.4 0.8 fusion.56
  33.3 0.9 fusion.50
  34.2 0.9 fusion.52
  35.8 112.5 %all-reduce.5.cloned.1.call-done = f32[64,512]{1,0:T(8,128)} async-done(((f32[64,512]{1,0:T(8,128)}), f32[64,512]{1,0:T(8,128)}) %all-reduce.5.cloned.1.call-update) | async-done | bytes 131088 | tf_op jit(solution)/shard_map/psum | solution.py:66
  148.4 1.3 fusion.72
  151.6 0.8 multiply_reduce_fusion.5
  152.7 31.3 %all_gather.9 = bf16[512,512]{1,0:T(8,128)(2,1)S(1)} all-gather(bf16[64,512]{1,0:T(8,128)(2,1)S(1)} %get-tuple-element.19), channel_id=1, replica_groups=mesh['hi'=4,'lo'=8] {'lo'}, dimensions={0}, use_global_device_ids=true | all-gather | bytes 589824 | tf_op jit(solution)/shard_map/all_gather | solution.py:82
  184.0 1.1 convolution_bitcast_fusion.2
  185.8 20.3 %reduce-scatter.4.cloned.1.call-done = f32[64,512]{1,0:T(8,128)} async-done(((f32[256,512]{1,0:T(8,128)}), f32[64,512]{1,0:T(8,128)}) %reduce-scatter.4.cloned.1.call-update) | async-done | bytes 131088 | tf_op jit(solution)/shard_map/reduce_scatter | solution.py:85
  206.1 2.2 multiply_reduce_fusion.4
  208.3 39.5 %all-reduce = (f32[512]{0:T(512)S(1)}, f32[512]{0:T(512)S(1)}) all-reduce(f32[512]{0:T(512)S(1)} %get-tuple-element.21, f32[512]{0:T(512)S(1)} %multiply_reduce_fusion.4), channel_id=1, replica_groups=mesh['hi'=4,'lo'=8] {'hi','lo'}, use_global_device_ids=true, to_apply=%region_1.0 | all-reduce | flops 1024 | bytes 8192 | tf_op jit(solution)/shard_map/psum | solution.py:66
  247.8 2.2 multiply_subtract_fusion.2
  249.9 1.1 fusion.151
  251.1 1.3 fusion.16
  252.4 1.4 fusion.14
  253.8 1.4 fusion.12
  255.1 1.4 fusion.10
  257.2 1.4 fusion.18
  258.6 1.5 collective-permute-start.6
  260.2 1.4 collective-permute-start.7
  261.7 2.3 collective-permute-start.9
  264.1 1.6 collective-permute-start.5
  265.6 117.0 %all-reduce.7.cloned.1.call-done = f32[64,512]{1,0:T(8,128)} async-done(((f32[64,512]{1,0:T(8,128)}), f32[64,512]{1,0:T(8,128)}) %all-reduce.7.cloned.1.call-update) | async-done | bytes 131088 | tf_op jit(solution)/shard_map/psum | solution.py:66
  382.6 1.3 fusion.66
  386.6 39.3 %psum.66 = f32[512]{0:T(512)S(1)} all-reduce(f32[512]{0:T(512)S(1)} %get-tuple-element.25), channel_id=1, replica_groups=mesh['hi'=4,'lo'=8] {'hi','lo'}, use_global_device_ids=true, to_apply=%region_8.9 | all-reduce | flops 512 | bytes 4096 | tf_op jit(solution)/shard_map/psum | solution.py:66
  426.1 31.2 %all_gather.10 = bf16[512,512]{1,0:T(8,128)(2,1)S(1)} all-gather(bf16[64,512]{1,0:T(8,128)(2,1)S(1)} %get-tuple-element.29), channel_id=1, replica_groups=mesh['hi'=4,'lo'=8] {'lo'}, dimensions={0}, use_global_device_ids=true | all-gather | bytes 589824 | tf_op jit(solution)/shard_map/all_gather | solution.py:82
  457.3 1.1 convolution_bitcast_fusion.1
  458.5 22.0 %reduce-scatter.6.cloned.1.call-done = f32[64,512]{1,0:T(8,128)} async-done(((f32[256,512]{1,0:T(8,128)}), f32[64,512]{1,0:T(8,128)}) %reduce-scatter.6.cloned.1.call-update) | async-done | bytes 131088 | tf_op jit(solution)/shard_map/reduce_scatter | solution.py:85
  480.5 2.2 multiply_reduce_fusion.2
  482.7 39.5 %psum.68 = f32[512]{0:T(512)S(1)} all-reduce(f32[512]{0:T(512)S(1)} %multiply_reduce_fusion.2), channel_id=1, replica_groups=mesh['hi'=4,'lo'=8] {'hi','lo'}, use_global_device_ids=true, to_apply=%region_13.14 | all-reduce | flops 512 | bytes 4096 | tf_op jit(solution)/shard_map/psum | solution.py:87
  522.2 2.2 multiply_subtract_fusion.1
  524.4 1.1 fusion.152
  525.6 1.3 fusion.6
  526.9 1.4 fusion.4
  528.2 1.4 fusion.2
  529.6 1.4 fusion
  531.7 1.4 fusion.8
  533.1 1.5 collective-permute-start.11
  534.7 1.4 collective-permute-start.12
  536.2 2.3 collective-permute-start.14
  538.5 1.5 collective-permute-start.10
  540.1 117.0 %all-reduce.9.cloned.1.call-done = f32[64,512]{1,0:T(8,128)} async-done(((f32[64,512]{1,0:T(8,128)}), f32[64,512]{1,0:T(8,128)}) %all-reduce.9.cloned.1.call-update) | async-done | bytes 131088 | tf_op jit(solution)/shard_map/psum | solution.py:66
  657.1 1.3 fusion.60
  660.2 0.8 multiply_reduce_fusion.1
  661.0 39.3 %psum.69 = f32[512]{0:T(512)S(1)} all-reduce(f32[512]{0:T(512)S(1)} %get-tuple-element.31), channel_id=1, replica_groups=mesh['hi'=4,'lo'=8] {'hi','lo'}, use_global_device_ids=true, to_apply=%region_15.16 | all-reduce | flops 512 | bytes 4096 | tf_op jit(solution)/shard_map/psum | solution.py:66
  700.6 31.2 %all_gather.11 = bf16[512,512]{1,0:T(8,128)(2,1)S(1)} all-gather(bf16[64,512]{1,0:T(8,128)(2,1)S(1)} %get-tuple-element.35), channel_id=1, replica_groups=mesh['hi'=4,'lo'=8] {'lo'}, dimensions={0}, use_global_device_ids=true | all-gather | bytes 589824 | tf_op jit(solution)/shard_map/all_gather | solution.py:82
  731.8 1.1 convolution_bitcast_fusion
  732.9 22.1 %reduce-scatter.8.cloned.1.call-done = f32[64,512]{1,0:T(8,128)} async-done(((f32[256,512]{1,0:T(8,128)}), f32[64,512]{1,0:T(8,128)}) %reduce-scatter.8.cloned.1.call-update) | async-done | bytes 131088 | tf_op jit(solution)/shard_map/reduce_scatter | solution.py:85
  755.1 2.2 multiply_reduce_fusion
  757.2 39.3 %psum.71 = f32[512]{0:T(512)S(1)} all-reduce(f32[512]{0:T(512)S(1)} %multiply_reduce_fusion), channel_id=1, replica_groups=mesh['hi'=4,'lo'=8] {'hi','lo'}, use_global_device_ids=true, to_apply=%region_20.21 | all-reduce | flops 512 | bytes 4096 | tf_op jit(solution)/shard_map/psum | solution.py:87
  796.6 2.9 multiply_subtract_fusion
  (110 shorter events, 14.3 us)
Async XLA Ops:
  7.2 176.8 %copy-start = (bf16[4,1,64,1,512]{4,2,3,1,0:T(8,128)(2,1)S(1)}, bf16[4,1,64,1,512]{4,2,3,1,0:T(8,128)(2,1)}, u32[]{:S(2)}) copy-start(bf16[4,1,64,1,512]{4,2,3,1,0:T(8,128)(2,1)} %param.8) | copy-start | bytes 786436
  7.2 141.2 %all-reduce.5.cloned.1.call-start = ((), (), s32[]{:S(2)}) async-start(), calls=%async_computation.3 | async-start | bytes 262144 | tf_op jit(solution)/shard_map/psum | solution.py:66
  12.1 137.5 %collective-permute-start.1 = (bf16[64,512]{1,0:T(8,128)(2,1)S(1)}, bf16[64,512]{1,0:T(8,128)(2,1)S(1)}, u32[]{:S(2)}, u32[]{:S(2)}) collective-permute-start(bf16[64,512]{1,0:T(8,128)(2,1)S(1)} %bitcast.372), channel_id=1, source_target_pairs={{0,2},{1,3},{2,0},{3,1},{4,6},{5,7},{6,4},{7,5},{8,10},{9,11},{10,... | collective-permute-start | bytes 196616 | tf_op jit(solution)/shard_map/ppermute | solution.py:12
  16.6 133.3 %collective-permute-start.2 = (bf16[64,512]{1,0:T(8,128)(2,1)S(1)}, bf16[64,512]{1,0:T(8,128)(2,1)S(1)}, u32[]{:S(2)}, u32[]{:S(2)}) collective-permute-start(bf16[64,512]{1,0:T(8,128)(2,1)S(1)} %bitcast.371), channel_id=1, source_target_pairs={{0,4},{1,5},{2,6},{3,7},{4,0},{5,1},{6,2},{7,3},{8,12},{9,13},{10,... | collective-permute-start | bytes 196616 | tf_op jit(solution)/shard_map/ppermute | solution.py:12
  20.7 129.5 %collective-permute-start.3 = (bf16[64,512]{1,0:T(8,128)(2,1)S(1)}, bf16[64,512]{1,0:T(8,128)(2,1)S(1)}, u32[]{:S(2)}, u32[]{:S(2)}) collective-permute-start(bf16[64,512]{1,0:T(8,128)(2,1)S(1)} %bitcast.370), channel_id=1, source_target_pairs={{0,8},{8,0},{16,24},{24,16},{1,9},{9,1},{17,25},{25,17},{2,10},{10... | collective-permute-start | bytes 196616 | tf_op jit(solution)/shard_map/ppermute | solution.py:12
  22.1 8.5 %copy-start.1 = (f32[9,64,64]{2,1,0:T(8,128)S(1)}, f32[9,64,64]{2,1,0:T(8,128)}, u32[]{:S(2)}) copy-start(f32[9,64,64]{2,1,0:T(8,128)} %param.12) | copy-start | bytes 442372
  22.1 128.4 %collective-permute-start.4 = (bf16[64,512]{1,0:T(8,128)(2,1)S(1)}, bf16[64,512]{1,0:T(8,128)(2,1)S(1)}, u32[]{:S(2)}, u32[]{:S(2)}) collective-permute-start(bf16[64,512]{1,0:T(8,128)(2,1)S(1)} %bitcast.368), channel_id=1, source_target_pairs={{0,16},{8,24},{16,0},{24,8},{1,17},{9,25},{17,1},{25,9},{2,18},{10... | collective-permute-start | bytes 196616 | tf_op jit(solution)/shard_map/ppermute | solution.py:12
  25.1 125.7 %collective-permute-start = (bf16[64,512]{1,0:T(8,128)(2,1)S(1)}, bf16[64,512]{1,0:T(8,128)(2,1)S(1)}, u32[]{:S(2)}, u32[]{:S(2)}) collective-permute-start(bf16[64,512]{1,0:T(8,128)(2,1)S(1)} %bitcast.369), channel_id=1, source_target_pairs={{0,1},{1,0},{2,3},{3,2},{4,5},{5,4},{6,7},{7,6},{8,9},{9,8},{10,11... | collective-permute-start | bytes 196616 | tf_op jit(solution)/shard_map/ppermute | solution.py:12
  27.4 178.7 %reduce-scatter.4.cloned.1.call-start = ((), (), s32[]{:S(2)}) async-start(), calls=%async_computation.4 | async-start | bytes 655360 | tf_op jit(solution)/shard_map/reduce_scatter | solution.py:85
  150.5 1.1 copy-start.2
  150.5 1.0 copy-start.3
  150.5 1.0 copy-start.5
  152.7 32.5 %copy-start.6 = (f32[2]{0:T(128)S(1)}, f32[2]{0:T(128)}, u32[]{:S(2)}) copy-start(f32[2]{0:T(128)} %param.14) | copy-start | bytes 28
  184.0 63.8 %copy-start.4 = (s32[512]{0:T(512)S(1)}, s32[512]{0:T(512)}, u32[]{:S(2)}) copy-start(s32[512]{0:T(512)} %param.15) | copy-start | bytes 6148
  185.1 197.5 %all-reduce.7.cloned.1.call-start = ((), (), s32[]{:S(2)}) async-start(), calls=%async_computation.5 | async-start | bytes 262144 | tf_op jit(solution)/shard_map/psum | solution.py:66
  257.2 223.3 %reduce-scatter.6.cloned.1.call-start = ((), (), s32[]{:S(2)}) async-start(), calls=%async_computation.6 | async-start | bytes 655360 | tf_op jit(solution)/shard_map/reduce_scatter | solution.py:85
  258.6 125.2 %collective-permute-start.6 = (bf16[64,512]{1,0:T(8,128)(2,1)S(1)}, bf16[64,512]{1,0:T(8,128)(2,1)S(1)}, u32[]{:S(2)}, u32[]{:S(2)}) collective-permute-start(bf16[64,512]{1,0:T(8,128)(2,1)S(1)} %bitcast.381), channel_id=1, source_target_pairs={{0,2},{1,3},{2,0},{3,1},{4,6},{5,7},{6,4},{7,5},{8,10},{9,11},{10,... | collective-permute-start | bytes 196616 | tf_op jit(solution)/shard_map/ppermute | solution.py:12
  260.2 124.0 %collective-permute-start.7 = (bf16[64,512]{1,0:T(8,128)(2,1)S(1)}, bf16[64,512]{1,0:T(8,128)(2,1)S(1)}, u32[]{:S(2)}, u32[]{:S(2)}) collective-permute-start(bf16[64,512]{1,0:T(8,128)(2,1)S(1)} %bitcast.380), channel_id=1, source_target_pairs={{0,4},{1,5},{2,6},{3,7},{4,0},{5,1},{6,2},{7,3},{8,12},{9,13},{10,... | collective-permute-start | bytes 196616 | tf_op jit(solution)/shard_map/ppermute | solution.py:12
  261.6 122.8 %collective-permute-start.8 = (bf16[64,512]{1,0:T(8,128)(2,1)S(1)}, bf16[64,512]{1,0:T(8,128)(2,1)S(1)}, u32[]{:S(2)}, u32[]{:S(2)}) collective-permute-start(bf16[64,512]{1,0:T(8,128)(2,1)S(1)} %bitcast.378), channel_id=1, source_target_pairs={{0,8},{8,0},{16,24},{24,16},{1,9},{9,1},{17,25},{25,17},{2,10},{10... | collective-permute-start | bytes 196616 | tf_op jit(solution)/shard_map/ppermute | solution.py:12
  261.7 123.0 %collective-permute-start.9 = (bf16[64,512]{1,0:T(8,128)(2,1)S(1)}, bf16[64,512]{1,0:T(8,128)(2,1)S(1)}, u32[]{:S(2)}, u32[]{:S(2)}) collective-permute-start(bf16[64,512]{1,0:T(8,128)(2,1)S(1)} %bitcast.376), channel_id=1, source_target_pairs={{0,16},{8,24},{16,0},{24,8},{1,17},{9,25},{17,1},{25,9},{2,18},{10... | collective-permute-start | bytes 196616 | tf_op jit(solution)/shard_map/ppermute | solution.py:12
  264.1 121.0 %collective-permute-start.5 = (bf16[64,512]{1,0:T(8,128)(2,1)S(1)}, bf16[64,512]{1,0:T(8,128)(2,1)S(1)}, u32[]{:S(2)}, u32[]{:S(2)}) collective-permute-start(bf16[64,512]{1,0:T(8,128)(2,1)S(1)} %bitcast.375), channel_id=1, source_target_pairs={{0,1},{1,0},{2,3},{3,2},{4,5},{5,4},{6,7},{7,6},{8,9},{9,8},{10,11... | collective-permute-start | bytes 196616 | tf_op jit(solution)/shard_map/ppermute | solution.py:12
  458.4 198.6 %all-reduce.9.cloned.1.call-start = ((), (), s32[]{:S(2)}) async-start(), calls=%async_computation.7 | async-start | bytes 262144 | tf_op jit(solution)/shard_map/psum | solution.py:66
  531.7 223.4 %reduce-scatter.8.cloned.1.call-start = ((), (), s32[]{:S(2)}) async-start(), calls=%async_computation.8 | async-start | bytes 655360 | tf_op jit(solution)/shard_map/reduce_scatter | solution.py:85
  533.1 125.2 %collective-permute-start.11 = (bf16[64,512]{1,0:T(8,128)(2,1)S(1)}, bf16[64,512]{1,0:T(8,128)(2,1)S(1)}, u32[]{:S(2)}, u32[]{:S(2)}) collective-permute-start(bf16[64,512]{1,0:T(8,128)(2,1)S(1)} %bitcast.382), channel_id=1, source_target_pairs={{0,2},{1,3},{2,0},{3,1},{4,6},{5,7},{6,4},{7,5},{8,10},{9,11},{10,... | collective-permute-start | bytes 196616 | tf_op jit(solution)/shard_map/ppermute | solution.py:12
  534.7 124.0 %collective-permute-start.12 = (bf16[64,512]{1,0:T(8,128)(2,1)S(1)}, bf16[64,512]{1,0:T(8,128)(2,1)S(1)}, u32[]{:S(2)}, u32[]{:S(2)}) collective-permute-start(bf16[64,512]{1,0:T(8,128)(2,1)S(1)} %bitcast.379), channel_id=1, source_target_pairs={{0,4},{1,5},{2,6},{3,7},{4,0},{5,1},{6,2},{7,3},{8,12},{9,13},{10,... | collective-permute-start | bytes 196616 | tf_op jit(solution)/shard_map/ppermute | solution.py:12
  536.1 122.8 %collective-permute-start.13 = (bf16[64,512]{1,0:T(8,128)(2,1)S(1)}, bf16[64,512]{1,0:T(8,128)(2,1)S(1)}, u32[]{:S(2)}, u32[]{:S(2)}) collective-permute-start(bf16[64,512]{1,0:T(8,128)(2,1)S(1)} %bitcast.377), channel_id=1, source_target_pairs={{0,8},{8,0},{16,24},{24,16},{1,9},{9,1},{17,25},{25,17},{2,10},{10... | collective-permute-start | bytes 196616 | tf_op jit(solution)/shard_map/ppermute | solution.py:12
  536.2 123.0 %collective-permute-start.14 = (bf16[64,512]{1,0:T(8,128)(2,1)S(1)}, bf16[64,512]{1,0:T(8,128)(2,1)S(1)}, u32[]{:S(2)}, u32[]{:S(2)}) collective-permute-start(bf16[64,512]{1,0:T(8,128)(2,1)S(1)} %bitcast.374), channel_id=1, source_target_pairs={{0,16},{8,24},{16,0},{24,8},{1,17},{9,25},{17,1},{25,9},{2,18},{10... | collective-permute-start | bytes 196616 | tf_op jit(solution)/shard_map/ppermute | solution.py:12
  538.5 120.9 %collective-permute-start.10 = (bf16[64,512]{1,0:T(8,128)(2,1)S(1)}, bf16[64,512]{1,0:T(8,128)(2,1)S(1)}, u32[]{:S(2)}, u32[]{:S(2)}) collective-permute-start(bf16[64,512]{1,0:T(8,128)(2,1)S(1)} %bitcast.373), channel_id=1, source_target_pairs={{0,1},{1,0},{2,3},{3,2},{4,5},{5,4},{6,7},{7,6},{8,9},{9,8},{10,11... | collective-permute-start | bytes 196616 | tf_op jit(solution)/shard_map/ppermute | solution.py:12
Sparse Core Ops, SparseCore 0:
  27.5 120.8 all-reduce.4
  185.2 20.8 reduce-scatter.3
  257.3 125.2 all-reduce.6
  458.6 21.9 reduce-scatter.5
  531.8 125.2 all-reduce.8
  733.1 21.9 reduce-scatter.7
where the time goes:
time: 808 us; the launch traced here: 806 us
  waiting for transfers between devices  411 us (51%)
  blocking collectives  291 us (36%)
  matrix products  43.6 us (5%)
  starting transfers between devices  23 us (3%)
  other arithmetic  18.3 us (2%)
  between operations  14.7 us (2%)
    psum x3, waiting for transfers between devices, precondition(): lax.psum((coefficients[level_total - 1], partial_energy), ('hi', 'lo'))  346 us
    psum x3, blocking collectives, precondition(): lax.psum((coefficients[level_total - 1], partial_energy), ('hi', 'lo'))  118 us
    all_gather x3, blocking collectives, local(): lax.all_gather(rounded, 'lo', axis=0, tiled=True)  93.7 us
    psum x2, blocking collectives, local(): curvature = lax.psum(jnp.sum(direction * image, axis=0), ('hi', 'lo'))  78.8 us
    reduce_scatter x3, waiting for transfers between devices, local(): lax.psum_scatter(partial_value, 'hi', scatter_dimension=0, tiled=True)  64.5 us
    ppermute x15, starting transfers between devices, from_partner(): return lax.ppermute(value, axis, pairs)  22.8 us
    dot_general x15, matrix products, level_pieces(): own_part = jnp.einsum('l,lrb->rb', select, coefficients)  20.4 us
  transfers between devices with their start and end apart: 21, of which 6 were waited for; matrix products, arithmetic and copies ran while one was open for 3% of the time, Pallas kernels for 0%

commit v1 on v0

--- a/solution.py
+++ b/solution.py
@@ -84,7 +84,9 @@
         )
         product = lax.psum_scatter(partial_value, "hi", scatter_dimension=0, tiled=True)
         image = genetic * product + noise * direction
-        curvature = lax.psum(jnp.sum(direction * image, axis=0), ("hi", "lo"))
+        curvature = jnp.sum(direction * image, axis=0)
+        for name in ("hi", "lo"):
+            curvature = lax.psum(curvature, name)
         alpha = energy / curvature
         stepsize = jnp.where(step < iters_per_column, alpha, jnp.zeros_like(alpha))
         solution = solution + stepsize * direction

time: 808 us -> 780 us (0.965)
  waiting for transfers between devices: 411 us -> 392 us
  starting transfers between devices: 23 us -> 14.4 us
    reduce_scatter x3, waiting for transfers between devices: 64.5 us -> 44.1 us  [local(): lax.psum_scatter(partial_value, 'hi', scatter_dimension=0, tiled=True)]
    ppermute x15, starting transfers between devices: 22.8 us -> 14.1 us  [from_partner(): return lax.ppermute(value, axis, pairs)]
    psum x2 -> x6, blocking collectives: 78.8 us -> 80.9 us  [local(): curvature = lax.psum(curvature, name)]
  transfers between devices with their start and end apart: 21 -> 21, of which waited for: 6 -> 5; matrix products, arithmetic and copies ran while one was open for 3% -> 3% of each run, Pallas kernels for 0% -> 0%
where the time goes in v1:
time: 780 us; the launch traced here: 779 us
  waiting for transfers between devices  392 us (50%)
  blocking collectives  291 us (37%)
  matrix products  43.6 us (6%)
  other arithmetic  18.3 us (2%)
  between operations  14.7 us (2%)
  starting transfers between devices  14.4 us (2%)
    psum x3, waiting for transfers between devices, precondition(): lax.psum((coefficients[level_total - 1], partial_energy), ('hi', 'lo'))  348 us
    psum x3, blocking collectives, precondition(): lax.psum((coefficients[level_total - 1], partial_energy), ('hi', 'lo'))  116 us
    all_gather x3, blocking collectives, local(): lax.all_gather(rounded, 'lo', axis=0, tiled=True)  93.7 us
    psum x6, blocking collectives, local(): curvature = lax.psum(curvature, name)  80.9 us
    reduce_scatter x3, waiting for transfers between devices, local(): lax.psum_scatter(partial_value, 'hi', scatter_dimension=0, tiled=True)  44.1 us
    dot_general x15, matrix products, level_pieces(): own_part = jnp.einsum('l,lrb->rb', select, coefficients)  20.4 us
  transfers between devices with their start and end apart: 21, of which 5 were waited for; matrix products, arithmetic and copies ran while one was open for 3% of the time, Pallas kernels for 0%

profile of v1, /device:TPU:0, one launch (start us, length us, event | category | flops | bytes accessed | tf_op | source)
XLA Modules:
  0.0 779.1 jit_solution(11061564961943452731)
XLA Ops:
  7.2 1.5 fusion.146
  8.7 2.1 fusion.150
  10.8 1.3 fusion.26
  12.1 3.1 collective-permute-start.1
  15.3 1.4 fusion.24
  16.6 2.7 collective-permute-start.2
  19.3 1.4 fusion.22
  20.8 1.4 fusion.20
  22.1 1.6 collective-permute-start.4
  23.7 1.4 fusion.28
  25.1 1.6 collective-permute-start
  30.6 0.9 fusion.58
  31.5 0.9 fusion.54
  32.4 0.8 fusion.56
  33.3 0.9 fusion.50
  34.2 0.9 fusion.52
  35.8 112.5 %all-reduce.4.cloned.1.call-done = f32[64,512]{1,0:T(8,128)} async-done(((f32[64,512]{1,0:T(8,128)}), f32[64,512]{1,0:T(8,128)}) %all-reduce.4.cloned.1.call-update) | async-done | bytes 131088 | tf_op jit(solution)/shard_map/psum | solution.py:66
  148.4 1.3 fusion.72
  151.6 0.8 multiply_reduce_fusion.5
  152.7 31.3 %all_gather.9 = bf16[512,512]{1,0:T(8,128)(2,1)S(1)} all-gather(bf16[64,512]{1,0:T(8,128)(2,1)S(1)} %get-tuple-element.17), channel_id=1, replica_groups=mesh['hi'=4,'lo'=8] {'lo'}, dimensions={0}, use_global_device_ids=true | all-gather | bytes 589824 | tf_op jit(solution)/shard_map/all_gather | solution.py:82
  184.0 1.1 convolution_bitcast_fusion.2
  185.8 37.7 %psum.84 = f32[512]{0:T(512)S(1)} all-reduce(f32[512]{0:T(512)S(1)} %get-tuple-element.19), channel_id=1, replica_groups=mesh['hi'=4,'lo'=8] {'hi','lo'}, use_global_device_ids=true, to_apply=%region_1.0 | all-reduce | flops 512 | bytes 4096 | tf_op jit(solution)/shard_map/psum | solution.py:66
  223.4 2.2 multiply_reduce_fusion.4
  225.6 6.7 psum.86
  232.3 19.5 %psum.87 = f32[512]{0:T(512)S(1)} all-reduce(f32[512]{0:T(512)S(1)} %psum.86), channel_id=1, replica_groups=mesh['hi'=4,'lo'=8] {'lo'}, use_global_device_ids=true, to_apply=%region_7.0 | all-reduce | flops 512 | bytes 4096 | tf_op jit(solution)/shard_map/psum | solution.py:89
  251.8 2.2 multiply_subtract_fusion.2
  254.0 1.1 fusion.151
  255.1 1.3 fusion.16
  256.4 1.4 fusion.14
  257.8 1.4 fusion.12
  259.2 1.4 fusion.10
  261.3 1.4 fusion.18
  263.0 1.8 collective-permute-start.9
  264.8 0.9 collective-permute-start.5
  265.7 117.7 %all-reduce.6.cloned.1.call-done = f32[64,512]{1,0:T(8,128)} async-done(((f32[64,512]{1,0:T(8,128)}), f32[64,512]{1,0:T(8,128)}) %all-reduce.6.cloned.1.call-update) | async-done | bytes 131088 | tf_op jit(solution)/shard_map/psum | solution.py:66
  383.4 1.3 fusion.66
  386.6 0.8 multiply_reduce_fusion.3
  387.4 39.2 %psum.88 = f32[512]{0:T(512)S(1)} all-reduce(f32[512]{0:T(512)S(1)} %get-tuple-element.23), channel_id=1, replica_groups=mesh['hi'=4,'lo'=8] {'hi','lo'}, use_global_device_ids=true, to_apply=%region_9.10 | all-reduce | flops 512 | bytes 4096 | tf_op jit(solution)/shard_map/psum | solution.py:66
  426.9 31.2 %all_gather.10 = bf16[512,512]{1,0:T(8,128)(2,1)S(1)} all-gather(bf16[64,512]{1,0:T(8,128)(2,1)S(1)} %get-tuple-element.27), channel_id=1, replica_groups=mesh['hi'=4,'lo'=8] {'lo'}, dimensions={0}, use_global_device_ids=true | all-gather | bytes 589824 | tf_op jit(solution)/shard_map/all_gather | solution.py:82
  458.2 1.1 convolution_bitcast_fusion.1
  459.3 22.0 %reduce-scatter.6.cloned.1.call-done = f32[64,512]{1,0:T(8,128)} async-done(((f32[256,512]{1,0:T(8,128)}), f32[64,512]{1,0:T(8,128)}) %reduce-scatter.6.cloned.1.call-update) | async-done | bytes 131088 | tf_op jit(solution)/shard_map/reduce_scatter | solution.py:85
  481.3 2.2 multiply_reduce_fusion.2
  483.5 5.8 psum.90
  489.2 21.7 %psum.91 = f32[512]{0:T(512)S(1)} all-reduce(f32[512]{0:T(512)S(1)} %psum.90), channel_id=1, replica_groups=mesh['hi'=4,'lo'=8] {'lo'}, use_global_device_ids=true, to_apply=%region_15.16 | all-reduce | flops 512 | bytes 4096 | tf_op jit(solution)/shard_map/psum | solution.py:89
  511.0 2.2 multiply_subtract_fusion.1
  513.2 1.1 fusion.152
  514.3 1.3 fusion.6
  515.6 1.4 fusion.4
  517.0 1.4 fusion.2
  518.3 1.4 fusion
  520.4 1.4 fusion.8
  522.1 1.1 collective-permute-start.14
  523.2 0.9 collective-permute-start.10
  524.1 117.7 %all-reduce.8.cloned.1.call-done = f32[64,512]{1,0:T(8,128)} async-done(((f32[64,512]{1,0:T(8,128)}), f32[64,512]{1,0:T(8,128)}) %all-reduce.8.cloned.1.call-update) | async-done | bytes 131088 | tf_op jit(solution)/shard_map/psum | solution.py:66
  641.9 1.3 fusion.60
  645.0 0.8 multiply_reduce_fusion.1
  645.8 39.3 %psum.92 = f32[512]{0:T(512)S(1)} all-reduce(f32[512]{0:T(512)S(1)} %get-tuple-element.29), channel_id=1, replica_groups=mesh['hi'=4,'lo'=8] {'hi','lo'}, use_global_device_ids=true, to_apply=%region_17.18 | all-reduce | flops 512 | bytes 4096 | tf_op jit(solution)/shard_map/psum | solution.py:66
  685.4 31.2 %all_gather.11 = bf16[512,512]{1,0:T(8,128)(2,1)S(1)} all-gather(bf16[64,512]{1,0:T(8,128)(2,1)S(1)} %get-tuple-element.33), channel_id=1, replica_groups=mesh['hi'=4,'lo'=8] {'lo'}, dimensions={0}, use_global_device_ids=true | all-gather | bytes 589824 | tf_op jit(solution)/shard_map/all_gather | solution.py:82
  716.6 1.1 convolution_bitcast_fusion
  717.8 22.1 %reduce-scatter.8.cloned.1.call-done = f32[64,512]{1,0:T(8,128)} async-done(((f32[256,512]{1,0:T(8,128)}), f32[64,512]{1,0:T(8,128)}) %reduce-scatter.8.cloned.1.call-update) | async-done | bytes 131088 | tf_op jit(solution)/shard_map/reduce_scatter | solution.py:85
  739.9 2.2 multiply_reduce_fusion
  742.1 5.8 psum.94
  747.8 21.5 %psum.95 = f32[512]{0:T(512)S(1)} all-reduce(f32[512]{0:T(512)S(1)} %psum.94), channel_id=1, replica_groups=mesh['hi'=4,'lo'=8] {'lo'}, use_global_device_ids=true, to_apply=%region_23.24 | all-reduce | flops 512 | bytes 4096 | tf_op jit(solution)/shard_map/psum | solution.py:89
  769.3 2.9 multiply_subtract_fusion
  (114 shorter events, 13.8 us)
Async XLA Ops:
  7.2 176.8 %copy-start = (bf16[4,1,64,1,512]{4,2,3,1,0:T(8,128)(2,1)S(1)}, bf16[4,1,64,1,512]{4,2,3,1,0:T(8,128)(2,1)}, u32[]{:S(2)}) copy-start(bf16[4,1,64,1,512]{4,2,3,1,0:T(8,128)(2,1)} %param.8) | copy-start | bytes 786436
  7.2 141.2 %all-reduce.4.cloned.1.call-start = ((), (), s32[]{:S(2)}) async-start(), calls=%async_computation.3 | async-start | bytes 262144 | tf_op jit(solution)/shard_map/psum | solution.py:66
  12.1 137.5 %collective-permute-start.1 = (bf16[64,512]{1,0:T(8,128)(2,1)S(1)}, bf16[64,512]{1,0:T(8,128)(2,1)S(1)}, u32[]{:S(2)}, u32[]{:S(2)}) collective-permute-start(bf16[64,512]{1,0:T(8,128)(2,1)S(1)} %bitcast.372), channel_id=1, source_target_pairs={{0,2},{1,3},{2,0},{3,1},{4,6},{5,7},{6,4},{7,5},{8,10},{9,11},{10,... | collective-permute-start | bytes 196616 | tf_op jit(solution)/shard_map/ppermute | solution.py:12
  16.6 133.3 %collective-permute-start.2 = (bf16[64,512]{1,0:T(8,128)(2,1)S(1)}, bf16[64,512]{1,0:T(8,128)(2,1)S(1)}, u32[]{:S(2)}, u32[]{:S(2)}) collective-permute-start(bf16[64,512]{1,0:T(8,128)(2,1)S(1)} %bitcast.371), channel_id=1, source_target_pairs={{0,4},{1,5},{2,6},{3,7},{4,0},{5,1},{6,2},{7,3},{8,12},{9,13},{10,... | collective-permute-start | bytes 196616 | tf_op jit(solution)/shard_map/ppermute | solution.py:12
  20.7 129.5 %collective-permute-start.3 = (bf16[64,512]{1,0:T(8,128)(2,1)S(1)}, bf16[64,512]{1,0:T(8,128)(2,1)S(1)}, u32[]{:S(2)}, u32[]{:S(2)}) collective-permute-start(bf16[64,512]{1,0:T(8,128)(2,1)S(1)} %bitcast.370), channel_id=1, source_target_pairs={{0,8},{8,0},{16,24},{24,16},{1,9},{9,1},{17,25},{25,17},{2,10},{10... | collective-permute-start | bytes 196616 | tf_op jit(solution)/shard_map/ppermute | solution.py:12
  22.1 8.5 %copy-start.1 = (f32[9,64,64]{2,1,0:T(8,128)S(1)}, f32[9,64,64]{2,1,0:T(8,128)}, u32[]{:S(2)}) copy-start(f32[9,64,64]{2,1,0:T(8,128)} %param.12) | copy-start | bytes 442372
  22.1 128.4 %collective-permute-start.4 = (bf16[64,512]{1,0:T(8,128)(2,1)S(1)}, bf16[64,512]{1,0:T(8,128)(2,1)S(1)}, u32[]{:S(2)}, u32[]{:S(2)}) collective-permute-start(bf16[64,512]{1,0:T(8,128)(2,1)S(1)} %bitcast.368), channel_id=1, source_target_pairs={{0,16},{8,24},{16,0},{24,8},{1,17},{9,25},{17,1},{25,9},{2,18},{10... | collective-permute-start | bytes 196616 | tf_op jit(solution)/shard_map/ppermute | solution.py:12
  25.1 125.7 %collective-permute-start = (bf16[64,512]{1,0:T(8,128)(2,1)S(1)}, bf16[64,512]{1,0:T(8,128)(2,1)S(1)}, u32[]{:S(2)}, u32[]{:S(2)}) collective-permute-start(bf16[64,512]{1,0:T(8,128)(2,1)S(1)} %bitcast.369), channel_id=1, source_target_pairs={{0,1},{1,0},{2,3},{3,2},{4,5},{5,4},{6,7},{7,6},{8,9},{9,8},{10,11... | collective-permute-start | bytes 196616 | tf_op jit(solution)/shard_map/ppermute | solution.py:12
  27.4 196.1 %reduce-scatter.4.cloned.1.call-start = ((), (), s32[]{:S(2)}) async-start(), calls=%async_computation.4 | async-start | bytes 655360 | tf_op jit(solution)/shard_map/reduce_scatter | solution.py:85
  150.5 1.1 copy-start.2
  150.5 1.0 copy-start.3
  150.5 1.0 copy-start.5
  152.7 32.5 %copy-start.6 = (f32[2]{0:T(128)S(1)}, f32[2]{0:T(128)}, u32[]{:S(2)}) copy-start(f32[2]{0:T(128)} %param.14) | copy-start | bytes 28
  184.0 67.8 %copy-start.4 = (s32[512]{0:T(512)S(1)}, s32[512]{0:T(512)}, u32[]{:S(2)}) copy-start(s32[512]{0:T(512)} %param.15) | copy-start | bytes 6148
  185.1 198.3 %all-reduce.6.cloned.1.call-start = ((), (), s32[]{:S(2)}) async-start(), calls=%async_computation.5 | async-start | bytes 262144 | tf_op jit(solution)/shard_map/psum | solution.py:66
  261.2 220.1 %reduce-scatter.6.cloned.1.call-start = ((), (), s32[]{:S(2)}) async-start(), calls=%async_computation.6 | async-start | bytes 655360 | tf_op jit(solution)/shard_map/reduce_scatter | solution.py:85
  262.7 122.0 %collective-permute-start.6 = (bf16[64,512]{1,0:T(8,128)(2,1)S(1)}, bf16[64,512]{1,0:T(8,128)(2,1)S(1)}, u32[]{:S(2)}, u32[]{:S(2)}) collective-permute-start(bf16[64,512]{1,0:T(8,128)(2,1)S(1)} %bitcast.381), channel_id=1, source_target_pairs={{0,2},{1,3},{2,0},{3,1},{4,6},{5,7},{6,4},{7,5},{8,10},{9,11},{10,... | collective-permute-start | bytes 196616 | tf_op jit(solution)/shard_map/ppermute | solution.py:12
  262.8 122.2 %collective-permute-start.7 = (bf16[64,512]{1,0:T(8,128)(2,1)S(1)}, bf16[64,512]{1,0:T(8,128)(2,1)S(1)}, u32[]{:S(2)}, u32[]{:S(2)}) collective-permute-start(bf16[64,512]{1,0:T(8,128)(2,1)S(1)} %bitcast.380), channel_id=1, source_target_pairs={{0,4},{1,5},{2,6},{3,7},{4,0},{5,1},{6,2},{7,3},{8,12},{9,13},{10,... | collective-permute-start | bytes 196616 | tf_op jit(solution)/shard_map/ppermute | solution.py:12
  262.9 122.4 %collective-permute-start.8 = (bf16[64,512]{1,0:T(8,128)(2,1)S(1)}, bf16[64,512]{1,0:T(8,128)(2,1)S(1)}, u32[]{:S(2)}, u32[]{:S(2)}) collective-permute-start(bf16[64,512]{1,0:T(8,128)(2,1)S(1)} %bitcast.378), channel_id=1, source_target_pairs={{0,8},{8,0},{16,24},{24,16},{1,9},{9,1},{17,25},{25,17},{2,10},{10... | collective-permute-start | bytes 196616 | tf_op jit(solution)/shard_map/ppermute | solution.py:12
  263.0 122.6 %collective-permute-start.9 = (bf16[64,512]{1,0:T(8,128)(2,1)S(1)}, bf16[64,512]{1,0:T(8,128)(2,1)S(1)}, u32[]{:S(2)}, u32[]{:S(2)}) collective-permute-start(bf16[64,512]{1,0:T(8,128)(2,1)S(1)} %bitcast.376), channel_id=1, source_target_pairs={{0,16},{8,24},{16,0},{24,8},{1,17},{9,25},{17,1},{25,9},{2,18},{10... | collective-permute-start | bytes 196616 | tf_op jit(solution)/shard_map/ppermute | solution.py:12
  264.8 121.0 %collective-permute-start.5 = (bf16[64,512]{1,0:T(8,128)(2,1)S(1)}, bf16[64,512]{1,0:T(8,128)(2,1)S(1)}, u32[]{:S(2)}, u32[]{:S(2)}) collective-permute-start(bf16[64,512]{1,0:T(8,128)(2,1)S(1)} %bitcast.375), channel_id=1, source_target_pairs={{0,1},{1,0},{2,3},{3,2},{4,5},{5,4},{6,7},{7,6},{8,9},{9,8},{10,11... | collective-permute-start | bytes 196616 | tf_op jit(solution)/shard_map/ppermute | solution.py:12
  459.3 182.6 %all-reduce.8.cloned.1.call-start = ((), (), s32[]{:S(2)}) async-start(), calls=%async_computation.7 | async-start | bytes 262144 | tf_op jit(solution)/shard_map/psum | solution.py:66
  520.4 219.5 %reduce-scatter.8.cloned.1.call-start = ((), (), s32[]{:S(2)}) async-start(), calls=%async_computation.8 | async-start | bytes 655360 | tf_op jit(solution)/shard_map/reduce_scatter | solution.py:85
  521.8 121.3 %collective-permute-start.11 = (bf16[64,512]{1,0:T(8,128)(2,1)S(1)}, bf16[64,512]{1,0:T(8,128)(2,1)S(1)}, u32[]{:S(2)}, u32[]{:S(2)}) collective-permute-start(bf16[64,512]{1,0:T(8,128)(2,1)S(1)} %bitcast.382), channel_id=1, source_target_pairs={{0,2},{1,3},{2,0},{3,1},{4,6},{5,7},{6,4},{7,5},{8,10},{9,11},{10,... | collective-permute-start | bytes 196616 | tf_op jit(solution)/shard_map/ppermute | solution.py:12
  521.9 121.5 %collective-permute-start.12 = (bf16[64,512]{1,0:T(8,128)(2,1)S(1)}, bf16[64,512]{1,0:T(8,128)(2,1)S(1)}, u32[]{:S(2)}, u32[]{:S(2)}) collective-permute-start(bf16[64,512]{1,0:T(8,128)(2,1)S(1)} %bitcast.379), channel_id=1, source_target_pairs={{0,4},{1,5},{2,6},{3,7},{4,0},{5,1},{6,2},{7,3},{8,12},{9,13},{10,... | collective-permute-start | bytes 196616 | tf_op jit(solution)/shard_map/ppermute | solution.py:12
  522.0 121.7 %collective-permute-start.13 = (bf16[64,512]{1,0:T(8,128)(2,1)S(1)}, bf16[64,512]{1,0:T(8,128)(2,1)S(1)}, u32[]{:S(2)}, u32[]{:S(2)}) collective-permute-start(bf16[64,512]{1,0:T(8,128)(2,1)S(1)} %bitcast.377), channel_id=1, source_target_pairs={{0,8},{8,0},{16,24},{24,16},{1,9},{9,1},{17,25},{25,17},{2,10},{10... | collective-permute-start | bytes 196616 | tf_op jit(solution)/shard_map/ppermute | solution.py:12
  522.1 121.9 %collective-permute-start.14 = (bf16[64,512]{1,0:T(8,128)(2,1)S(1)}, bf16[64,512]{1,0:T(8,128)(2,1)S(1)}, u32[]{:S(2)}, u32[]{:S(2)}) collective-permute-start(bf16[64,512]{1,0:T(8,128)(2,1)S(1)} %bitcast.374), channel_id=1, source_target_pairs={{0,16},{8,24},{16,0},{24,8},{1,17},{9,25},{17,1},{25,9},{2,18},{10... | collective-permute-start | bytes 196616 | tf_op jit(solution)/shard_map/ppermute | solution.py:12
  523.2 121.0 %collective-permute-start.10 = (bf16[64,512]{1,0:T(8,128)(2,1)S(1)}, bf16[64,512]{1,0:T(8,128)(2,1)S(1)}, u32[]{:S(2)}, u32[]{:S(2)}) collective-permute-start(bf16[64,512]{1,0:T(8,128)(2,1)S(1)} %bitcast.373), channel_id=1, source_target_pairs={{0,1},{1,0},{2,3},{3,2},{4,5},{5,4},{6,7},{7,6},{8,9},{9,8},{10,11... | collective-permute-start | bytes 196616 | tf_op jit(solution)/shard_map/ppermute | solution.py:12
Sparse Core Ops, SparseCore 0:
  27.5 120.8 all-reduce.3
  185.2 20.8 reduce-scatter.3
  261.3 122.0 all-reduce.5
  459.4 21.8 reduce-scatter.5
  520.5 121.3 all-reduce.7
  717.9 21.9 reduce-scatter.7
